TPU v7x, 32 devices: a whole 2x2x4 slice. The times are simulated.
32 devices in a mesh: gx: 4 (over y, x), gy: 4 (over z), gz: 2 (over core).
Axes of the slice: x: 2, y: 2, z: 4, core: 2. Of those that a mesh axis runs over, the one named last changes fastest.
Arguments:
- load: float32 [256, 256, 256], P('gx', 'gy', 'gz'), may hold values from -12 to 12
- stiffness: float32 [256, 256, 256], P('gx', 'gy', 'gz'), may hold values from 0.02 to 2
- prestress: float32 [256, 256], P(('gx', 'gy'), 'gz'), may hold values from -3 to 3
- state_var: float32 [256, 256], P(('gx', 'gy'), 'gz'), may hold values from -1 to 1
- normal_a: float32 [256, 256], P(('gx', 'gy'), 'gz'), may hold values from 1 to 3
Outputs:
- displacement: float32 [256, 256, 256], P('gx', 'gy', 'gz')
- slip_rate: float32 [256, 256], P(('gx', 'gy'), 'gz')
All inputs are finite; a program needn't handle non-finite values.
Results may differ from a plain program's by a relative error of at most 0.0003.
Values sent between devices are 32-bit elements; how exact they have to be, the bound alone decides.
A program may use at most 128 MiB of HBM per device.

v0:
```python
import jax
import jax.numpy as jnp
from jax import lax
from jax.sharding import PartitionSpec as P

ITERS = 3


def extended(cells, sides, width):
    for axis, dim in sides:
        count = lax.axis_size(axis)
        ends = count - 1
        head = lax.slice_in_dim(cells, 0, width, axis=dim)
        tail = lax.slice_in_dim(cells, cells.shape[dim] - width, cells.shape[dim], axis=dim)
        cells = jnp.concatenate(
            [
                lax.ppermute(tail, axis, [(i, (i + 1) % count) for i in range(ends)]),
                cells,
                lax.ppermute(head, axis, [((i + 1) % count, i) for i in range(ends)]),
            ],
            axis=dim,
        )
    return cells


def shifted(padded, sizes_now, axis_num, offset):
    slicers = [slice(2, 2 + sizes_now[0]), slice(2, 2 + sizes_now[1]), slice(2, 2 + sizes_now[2])]
    slicers[axis_num] = slice(2 + offset, 2 + offset + sizes_now[axis_num])
    return padded[tuple(slicers)]


def operate(field, stiffness):
    padded = extended(field, (("gx", 0), ("gy", 1), ("gz", 2)), 2)
    sizes_now = field.shape
    near_sum = jnp.zeros_like(field)
    for axis_num in range(3):
        near_sum = near_sum + 16.0 * (
            shifted(padded, sizes_now, axis_num, 1) + shifted(padded, sizes_now, axis_num, -1)
        )
        near_sum = near_sum - (
            shifted(padded, sizes_now, axis_num, 2) + shifted(padded, sizes_now, axis_num, -2)
        )
    return (7.5 + stiffness) * field - near_sum / 12.0


def paired_sums(residual, precond, image):
    return lax.psum((jnp.sum(residual * precond), jnp.sum(image * precond)), ("gx", "gy", "gz"))


def per_device(load, stiffness, prestress, state_var, normal_a):
    inverse = 1.0 / (7.5 + stiffness)
    solution = jnp.zeros_like(load)
    residual = load
    precond = inverse * residual
    image = operate(precond, stiffness)
    gamma, delta = paired_sums(residual, precond, image)
    alpha = gamma / delta
    direction = precond
    along = image
    for iteration in range(ITERS):
        solution = solution + alpha * direction
        residual = residual - alpha * along
        if iteration + 1 < ITERS:
            precond = inverse * residual
            image = operate(precond, stiffness)
            gamma_new, delta = paired_sums(residual, precond, image)
            ratio = gamma_new / gamma
            alpha = gamma_new / (delta - ratio * gamma_new / alpha)
            direction = precond + ratio * direction
            along = image + ratio * along
            gamma = gamma_new
    rows_y = solution.shape[1]
    total_y = rows_y * lax.axis_size("gy")
    edge_rows = jnp.concatenate((solution[:, :2, :], solution[:, rows_y - 2 :, :]), axis=1)
    local_rows = jnp.array([0, 1, rows_y - 2, rows_y - 1], dtype=jnp.int32)
    global_y = lax.axis_index("gy") * rows_y + local_rows
    offset = global_y - (total_y // 2 - 2)
    weights = (
        (offset == 0).astype(jnp.float32)
        - 27.0 * (offset == 1).astype(jnp.float32)
        + 27.0 * (offset == 2).astype(jnp.float32)
        - (offset == 3).astype(jnp.float32)
    ) / 24.0
    fault_term = jnp.sum(edge_rows * weights[None, :, None], axis=1)
    owned_rows = solution.shape[0] // lax.axis_size("gy")
    whole_strip = lax.psum(fault_term, "gy")
    traction = lax.dynamic_slice_in_dim(
        whole_strip, lax.axis_index("gy") * owned_rows, owned_rows, 0
    )
    slip_rate = jnp.exp(-state_var) * jnp.sinh((prestress + 2.0 * traction) / normal_a)
    return (solution, slip_rate)


def solution(mesh):
    placed = (
        P("gx", "gy", "gz"),
        P("gx", "gy", "gz"),
        P(("gx", "gy"), "gz"),
        P(("gx", "gy"), "gz"),
        P(("gx", "gy"), "gz"),
    )
    return jax.shard_map(
        per_device,
        mesh=mesh,
        in_specs=placed,
        out_specs=(P("gx", "gy", "gz"), P(("gx", "gy"), "gz")),
        check_vma=False,
    )
```

profile of v0, /device:TPU:0, one launch (start us, length us, event | category | flops | bytes accessed | tf_op | source)
XLA Modules:
  0.0 352.4 jit_solution(6903636222099214039)
XLA Ops:
  0.6 4.7 %copy_multiply_fusion = f32[64,64,128]{2,0,1:T(8,128)S(1)} fusion(f32[64,64,128]{2,1,0:T(8,128)} %param.6, f32[64,64,128]{2,1,0:T(8,128)} %param.7), kind=kLoop, calls=%fused_computation.122 | loop fusion | flops 1572864 | bytes 6291456 | tf_op jit(solution)/shard_map/mul | solution.py:54
  5.3 1.3 collective-permute-start
  6.6 5.5 %collective-permute-start.1 = (f32[2,64,128]{2,0,1:T(2,128)S(1)}, f32[2,64,128]{2,0,1:T(2,128)S(1)}, u32[]{:S(2)}, u32[]{:S(2)}) collective-permute-start(f32[2,64,128]{2,0,1:T(2,128)S(1)} %get-tuple-element.48), channel_id=1, source_target_pairs={{0,8},{8,16},{16,24},{1,9},{9,17},{17,25},{2,10},{10,18},{18,26},{... | collective-permute-start | bytes 196616 | tf_op jit(solution)/shard_map/ppermute | solution.py:17
  12.2 0.3 collective-permute-done
  12.5 1.6 collective-permute-done.1
  14.1 1.3 collective-permute-start.2
  15.4 4.6 %collective-permute-start.3 = (f32[68,2,128]{2,0,1:T(8,128)S(1)}, f32[68,2,128]{2,0,1:T(8,128)S(1)}, u32[]{:S(2)}, u32[]{:S(2)}) collective-permute-start(f32[68,2,128]{2,0,1:T(8,128)S(1)} %get-tuple-element.40), channel_id=1, source_target_pairs={{0,2},{2,4},{4,6},{1,3},{3,5},{5,7},{8,10},{10,12},{12,14},{9,11},... | collective-permute-start | bytes 208904 | tf_op jit(solution)/shard_map/ppermute | solution.py:17
  20.0 0.4 collective-permute-done.2
  20.4 1.6 collective-permute-done.3
  22.0 0.4 pad_maximum_fusion
  22.3 3.0 fusion.63
  25.3 2.6 copy.112
  27.9 1.3 collective-permute-start.5
  29.2 2.6 copy.110
  31.8 1.3 collective-permute-start.4
  33.1 2.6 pad_maximum_fusion.3
  35.8 2.4 copy.113
  38.2 2.4 copy.111
  40.6 13.9 %multiply_reduce_fusion.3 = (f32[]{:T(128)}, f32[]{:T(128)}, f32[64,64,128]{2,0,1:T(8,128)}) fusion(f32[64,64,128]{2,0,1:T(8,128)S(1)} %copy_multiply_fusion, f32[64,64,128]{2,1,0:T(8,128)} %param.6, f32[68,2,128]{2,0,1:T(8,128)S(1)} %collective-permute-done.2, f32[2,64,128]{2,0,1:T(2,128)S(1)} %collective-permute-done, ...), kind=kLoop, calls=%fused_computation.119 | loop fusion | flops 24117248 | bytes 17121544 | tf_op jit(solution)/shard_map/reduce_sum | solution.py:47
  54.5 44.4 %all-reduce.2 = (f32[]{:T(128)}, f32[]{:T(128)}) all-reduce(f32[]{:T(128)} %get-tuple-element.13, f32[]{:T(128)} %get-tuple-element.12), channel_id=1, replica_groups=mesh['gx'=4,'gy'=4,'gz'=2] {'gx','gy','gz'}, use_global_device_ids=true, to_apply=%region_1.0 | all-reduce | flops 2 | bytes 16 | tf_op jit(solution)/shard_map/psum | solution.py:47
  100.3 5.3 %fusion.48 = f32[64,64,128]{2,0,1:T(8,128)S(1)} fusion(f32[64,64,128]{2,0,1:T(8,128)} %get-tuple-element.23, f32[]{:T(128)S(6)} %div.45, f32[64,64,128]{2,1,0:T(8,128)} %param.6, f32[64,64,128]{2,1,0:T(8,128)} %param.7), kind=kLoop, calls=%fused_computation.124 | loop fusion | flops 2621440 | bytes 8388612 | tf_op jit(solution)/shard_map/mul | solution.py:64
  105.7 1.3 collective-permute-start.6
  107.0 4.8 %collective-permute-start.7 = (f32[2,64,128]{2,0,1:T(2,128)S(1)}, f32[2,64,128]{2,0,1:T(2,128)S(1)}, u32[]{:S(2)}, u32[]{:S(2)}) collective-permute-start(f32[2,64,128]{2,0,1:T(2,128)S(1)} %get-tuple-element.46), channel_id=1, source_target_pairs={{0,8},{8,16},{16,24},{1,9},{9,17},{17,25},{2,10},{10,18},{18,26},{... | collective-permute-start | bytes 196616 | tf_op jit(solution)/shard_map/ppermute | solution.py:17
  112.1 1.6 collective-permute-done.7
  113.7 1.3 collective-permute-start.8
  115.0 4.5 %collective-permute-start.9 = (f32[68,2,128]{2,0,1:T(8,128)S(1)}, f32[68,2,128]{2,0,1:T(8,128)S(1)}, u32[]{:S(2)}, u32[]{:S(2)}) collective-permute-start(f32[68,2,128]{2,0,1:T(8,128)S(1)} %get-tuple-element.36), channel_id=1, source_target_pairs={{0,2},{2,4},{4,6},{1,3},{3,5},{5,7},{8,10},{10,12},{12,14},{9,11},... | collective-permute-start | bytes 208904 | tf_op jit(solution)/shard_map/ppermute | solution.py:17
  119.6 0.4 collective-permute-done.8
  120.0 1.6 collective-permute-done.9
  121.5 0.4 pad_maximum_fusion.1
  121.9 3.0 fusion.62
  124.9 2.6 copy.117
  127.5 1.3 collective-permute-start.11
  128.8 2.6 copy.115
  131.4 1.3 collective-permute-start.10
  132.7 5.0 %pad_maximum_fusion.4 = (f32[68,66,128]{2,0,1:T(8,128)}, f32[68,66,128]{2,0,1:T(8,128)}) fusion(f32[68,2,128]{2,0,1:T(8,128)S(1)} %collective-permute-done.8, f32[2,64,128]{2,0,1:T(2,128)S(1)} %collective-permute-done.6, f32[64,64,128]{2,0,1:T(8,128)} %copy-done.1, f32[2,64,128]{2,0,1:T(2,128)S(1)} %collective-permute-done.7, ...), kind=kLoop, calls=%fused_computation.5 | loop fusion | flops 3446784 | bytes 6963200 | tf_op jit(solution)/shard_map/concatenate | solution.py:15
  137.7 2.4 copy.118
  140.1 2.4 copy.116
  142.5 22.0 %multiply_reduce_fusion.1 = (f32[]{:T(128)}, f32[]{:T(128)}, f32[64,64,128]{2,0,1:T(8,128)}) fusion(f32[64,64,128]{2,0,1:T(8,128)} %copy-done.1, f32[64,64,128]{2,0,1:T(8,128)} %get-tuple-element.23, f32[]{:T(128)S(6)} %div.45, f32[64,64,128]{2,1,0:T(8,128)} %param.6, f32[68,2,128]{2,0,1:T(8,128)S(1)} %collective-permute-done.8, ...), kind=kLoop, calls=%fused_computation.116 | loop fusion | flops 25165824 | bytes 19218700 | tf_op jit(solution)/shard_map/reduce_sum | solution.py:47
  164.5 44.4 %all-reduce.1 = (f32[]{:T(128)}, f32[]{:T(128)}) all-reduce(f32[]{:T(128)} %get-tuple-element.11, f32[]{:T(128)} %get-tuple-element.10), channel_id=1, replica_groups=mesh['gx'=4,'gy'=4,'gz'=2] {'gx','gy','gz'}, use_global_device_ids=true, to_apply=%region_5.0 | all-reduce | flops 2 | bytes 16 | tf_op jit(solution)/shard_map/psum | solution.py:47
  213.5 6.6 %multiply_reduce_fusion = (f32[]{:T(128)}, f32[64,64,128]{2,0,1:T(8,128)S(1)}) fusion(f32[64,64,128]{2,1,0:T(8,128)} %param.7, f32[64,64,128]{2,0,1:T(8,128)} %get-tuple-element.22, f32[64,64,128]{2,0,1:T(8,128)} %get-tuple-element.23, f32[]{:T(128)S(6)} %div.47, f32[]{:T(128)S(6)} %div.49, f32[]{:T(128)S(6)} %div.45, f32[64,64,128]{2,1,0:T(8,128)} %param.6), kind=kLoop, calls=%fused_computation.114 | loop fusion | flops 5767167 | bytes 10485776 | tf_op jit(solution)/shard_map/reduce_sum | solution.py:47
  220.1 1.3 copy-done
  221.5 1.3 collective-permute-start.12
  222.8 4.8 %collective-permute-start.13 = (f32[2,64,128]{2,0,1:T(2,128)S(1)}, f32[2,64,128]{2,0,1:T(2,128)S(1)}, u32[]{:S(2)}, u32[]{:S(2)}) collective-permute-start(f32[2,64,128]{2,0,1:T(2,128)S(1)} %get-tuple-element.44), channel_id=1, source_target_pairs={{0,8},{8,16},{16,24},{1,9},{9,17},{17,25},{2,10},{10,18},{18,26},{... | collective-permute-start | bytes 196616 | tf_op jit(solution)/shard_map/ppermute | solution.py:17
  227.9 1.6 collective-permute-done.13
  229.5 0.9 pad_maximum_fusion.42
  230.4 1.3 collective-permute-start.14
  231.7 4.5 %collective-permute-start.15 = (f32[68,2,128]{2,0,1:T(8,128)S(1)}, f32[68,2,128]{2,0,1:T(8,128)S(1)}, u32[]{:S(2)}, u32[]{:S(2)}) collective-permute-start(f32[68,2,128]{2,0,1:T(8,128)S(1)} %get-tuple-element.32), channel_id=1, source_target_pairs={{0,2},{2,4},{4,6},{1,3},{3,5},{5,7},{8,10},{10,12},{12,14},{9,11},... | collective-permute-start | bytes 208904 | tf_op jit(solution)/shard_map/ppermute | solution.py:17
  236.3 0.4 collective-permute-done.14
  236.7 1.6 collective-permute-done.15
  238.2 1.8 pad_maximum_fusion.2
  240.1 3.0 fusion.61
  243.1 2.6 copy.121
  245.7 1.3 collective-permute-start.17
  247.0 2.6 copy.119
  249.6 1.3 collective-permute-start.16
  250.9 5.0 %pad_maximum_fusion.5 = (f32[68,66,128]{2,0,1:T(8,128)}, f32[68,66,128]{2,0,1:T(8,128)}) fusion(f32[68,2,128]{2,0,1:T(8,128)S(1)} %collective-permute-done.14, f32[2,64,128]{2,0,1:T(2,128)S(1)} %collective-permute-done.12, f32[64,64,128]{2,0,1:T(8,128)} %copy-done, f32[2,64,128]{2,0,1:T(2,128)S(1)} %collective-permute-done.13, ...), kind=kLoop, calls=%fused_computation.7 | loop fusion | flops 3446784 | bytes 6963200 | tf_op jit(solution)/shard_map/concatenate | solution.py:15
  255.9 2.4 copy.122
  258.3 2.4 copy.120
  260.7 19.1 %fusion.46 = f32[]{:T(128)} fusion(f32[64,64,128]{2,0,1:T(8,128)} %copy-done, f32[68,2,128]{2,0,1:T(8,128)S(1)} %collective-permute-done.14, f32[2,64,128]{2,0,1:T(2,128)S(1)} %collective-permute-done.12, f32[2,64,128]{2,0,1:T(2,128)S(1)} %collective-permute-done.13, f32[68,2,128]{2,0,1:T(8,128)S(1)} %collective-permute-done.15, f32[68,68,2]{2,0,1:T(8,128)} %copy.122, ...), kind=kLoop, calls=%fused_computation.121 | loop fusion | flops 23068672 | bytes 12927236 | tf_op jit(solution)/shard_map/reduce_sum | solution.py:47
  279.8 44.4 %all-reduce = (f32[]{:T(128)}, f32[]{:T(128)}) all-reduce(f32[]{:T(128)} %get-tuple-element.20, f32[]{:T(128)} %fusion.46), channel_id=1, replica_groups=mesh['gx'=4,'gy'=4,'gz'=2] {'gx','gy','gz'}, use_global_device_ids=true, to_apply=%region_9.0 | all-reduce | flops 2 | bytes 16 | tf_op jit(solution)/shard_map/psum | solution.py:47
  328.1 3.0 multiply_add_fusion
  331.1 2.5 copy.125
  333.8 17.9 %psum.55 = f32[64,128]{1,0:T(8,128)S(1)} all-reduce(f32[64,128]{1,0:T(8,128)S(1)} %fusion.49), channel_id=1, replica_groups=mesh['gx'=4,'gy'=4,'gz'=2] {'gy'}, use_global_device_ids=true, to_apply=%region_13.0 | all-reduce | flops 8192 | bytes 65536 | tf_op jit(solution)/shard_map/psum | solution.py:86
  351.7 0.6 fusion.52
  (27 shorter events, 0.9 us)
Async XLA Ops:
  5.3 7.1 %collective-permute-start = (f32[2,64,128]{2,0,1:T(2,128)S(1)}, f32[2,64,128]{2,0,1:T(2,128)S(1)}, u32[]{:S(2)}, u32[]{:S(2)}) collective-permute-start(f32[2,64,128]{2,0,1:T(2,128)S(1)} %get-tuple-element.49), channel_id=1, source_target_pairs={{8,0},{16,8},{24,16},{9,1},{17,9},{25,17},{10,2},{18,10},{26,18},{... | collective-permute-start | bytes 196616 | tf_op jit(solution)/shard_map/ppermute | solution.py:19
  6.6 7.4 %collective-permute-start.1 = (f32[2,64,128]{2,0,1:T(2,128)S(1)}, f32[2,64,128]{2,0,1:T(2,128)S(1)}, u32[]{:S(2)}, u32[]{:S(2)}) collective-permute-start(f32[2,64,128]{2,0,1:T(2,128)S(1)} %get-tuple-element.48), channel_id=1, source_target_pairs={{0,8},{8,16},{16,24},{1,9},{9,17},{17,25},{2,10},{10,18},{18,26},{... | collective-permute-start | bytes 196616 | tf_op jit(solution)/shard_map/ppermute | solution.py:17
  14.1 6.3 %collective-permute-start.2 = (f32[68,2,128]{2,0,1:T(8,128)S(1)}, f32[68,2,128]{2,0,1:T(8,128)S(1)}, u32[]{:S(2)}, u32[]{:S(2)}) collective-permute-start(f32[68,2,128]{2,0,1:T(8,128)S(1)} %get-tuple-element.41), channel_id=1, source_target_pairs={{2,0},{4,2},{6,4},{3,1},{5,3},{7,5},{10,8},{12,10},{14,12},{11,9},... | collective-permute-start | bytes 208904 | tf_op jit(solution)/shard_map/ppermute | solution.py:19
  15.4 6.6 %collective-permute-start.3 = (f32[68,2,128]{2,0,1:T(8,128)S(1)}, f32[68,2,128]{2,0,1:T(8,128)S(1)}, u32[]{:S(2)}, u32[]{:S(2)}) collective-permute-start(f32[68,2,128]{2,0,1:T(8,128)S(1)} %get-tuple-element.40), channel_id=1, source_target_pairs={{0,2},{2,4},{4,6},{1,3},{3,5},{5,7},{8,10},{10,12},{12,14},{9,11},... | collective-permute-start | bytes 208904 | tf_op jit(solution)/shard_map/ppermute | solution.py:17
  27.9 7.8 %collective-permute-start.5 = (f32[68,68,2]{1,0,2:T(8,128)S(1)}, f32[68,68,2]{1,0,2:T(8,128)S(1)}, u32[]{:S(2)}, u32[]{:S(2)}) collective-permute-start(f32[68,68,2]{1,0,2:T(8,128)S(1)} %copy.112), channel_id=1, source_target_pairs={{0,1},{2,3},{4,5},{6,7},{8,9},{10,11},{12,13},{14,15},{16,17},{18,... | collective-permute-start | bytes 110984 | tf_op jit(solution)/shard_map/ppermute | solution.py:17
  31.8 6.3 %collective-permute-start.4 = (f32[68,68,2]{1,0,2:T(8,128)S(1)}, f32[68,68,2]{1,0,2:T(8,128)S(1)}, u32[]{:S(2)}, u32[]{:S(2)}) collective-permute-start(f32[68,68,2]{1,0,2:T(8,128)S(1)} %copy.110), channel_id=1, source_target_pairs={{1,0},{3,2},{5,4},{7,6},{9,8},{11,10},{13,12},{15,14},{17,16},{19,... | collective-permute-start | bytes 110984 | tf_op jit(solution)/shard_map/ppermute | solution.py:19
  105.6 15.9 %copy-start.1 = (f32[64,64,128]{2,0,1:T(8,128)}, f32[64,64,128]{2,0,1:T(8,128)S(1)}, u32[]{:S(2)}) copy-start(f32[64,64,128]{2,0,1:T(8,128)S(1)} %fusion.48) | copy-start | bytes 6291460
  105.7 6.4 %collective-permute-start.6 = (f32[2,64,128]{2,0,1:T(2,128)S(1)}, f32[2,64,128]{2,0,1:T(2,128)S(1)}, u32[]{:S(2)}, u32[]{:S(2)}) collective-permute-start(f32[2,64,128]{2,0,1:T(2,128)S(1)} %get-tuple-element.47), channel_id=1, source_target_pairs={{8,0},{16,8},{24,16},{9,1},{17,9},{25,17},{10,2},{18,10},{26,18},{... | collective-permute-start | bytes 196616 | tf_op jit(solution)/shard_map/ppermute | solution.py:19
  107.0 6.7 %collective-permute-start.7 = (f32[2,64,128]{2,0,1:T(2,128)S(1)}, f32[2,64,128]{2,0,1:T(2,128)S(1)}, u32[]{:S(2)}, u32[]{:S(2)}) collective-permute-start(f32[2,64,128]{2,0,1:T(2,128)S(1)} %get-tuple-element.46), channel_id=1, source_target_pairs={{0,8},{8,16},{16,24},{1,9},{9,17},{17,25},{2,10},{10,18},{18,26},{... | collective-permute-start | bytes 196616 | tf_op jit(solution)/shard_map/ppermute | solution.py:17
  113.7 6.2 %collective-permute-start.8 = (f32[68,2,128]{2,0,1:T(8,128)S(1)}, f32[68,2,128]{2,0,1:T(8,128)S(1)}, u32[]{:S(2)}, u32[]{:S(2)}) collective-permute-start(f32[68,2,128]{2,0,1:T(8,128)S(1)} %get-tuple-element.37), channel_id=1, source_target_pairs={{2,0},{4,2},{6,4},{3,1},{5,3},{7,5},{10,8},{12,10},{14,12},{11,9},... | collective-permute-start | bytes 208904 | tf_op jit(solution)/shard_map/ppermute | solution.py:19
  115.0 6.5 %collective-permute-start.9 = (f32[68,2,128]{2,0,1:T(8,128)S(1)}, f32[68,2,128]{2,0,1:T(8,128)S(1)}, u32[]{:S(2)}, u32[]{:S(2)}) collective-permute-start(f32[68,2,128]{2,0,1:T(8,128)S(1)} %get-tuple-element.36), channel_id=1, source_target_pairs={{0,2},{2,4},{4,6},{1,3},{3,5},{5,7},{8,10},{10,12},{12,14},{9,11},... | collective-permute-start | bytes 208904 | tf_op jit(solution)/shard_map/ppermute | solution.py:17
  127.5 10.2 %collective-permute-start.11 = (f32[68,68,2]{1,0,2:T(8,128)S(1)}, f32[68,68,2]{1,0,2:T(8,128)S(1)}, u32[]{:S(2)}, u32[]{:S(2)}) collective-permute-start(f32[68,68,2]{1,0,2:T(8,128)S(1)} %copy.117), channel_id=1, source_target_pairs={{0,1},{2,3},{4,5},{6,7},{8,9},{10,11},{12,13},{14,15},{16,17},{18,... | collective-permute-start | bytes 110984 | tf_op jit(solution)/shard_map/ppermute | solution.py:17
  131.4 8.7 %collective-permute-start.10 = (f32[68,68,2]{1,0,2:T(8,128)S(1)}, f32[68,68,2]{1,0,2:T(8,128)S(1)}, u32[]{:S(2)}, u32[]{:S(2)}) collective-permute-start(f32[68,68,2]{1,0,2:T(8,128)S(1)} %copy.115), channel_id=1, source_target_pairs={{1,0},{3,2},{5,4},{7,6},{9,8},{11,10},{13,12},{15,14},{17,16},{19,... | collective-permute-start | bytes 110984 | tf_op jit(solution)/shard_map/ppermute | solution.py:19
  220.1 1.3 copy-start
  220.1 16.1 %copy-start.5 = (s32[4]{0:T(128)S(1)}, s32[4]{0:T(128)}, u32[]{:S(2)}) copy-start(s32[4]{0:T(128)} %constant.51.clone) | copy-start | bytes 52
  221.5 6.4 %collective-permute-start.12 = (f32[2,64,128]{2,0,1:T(2,128)S(1)}, f32[2,64,128]{2,0,1:T(2,128)S(1)}, u32[]{:S(2)}, u32[]{:S(2)}) collective-permute-start(f32[2,64,128]{2,0,1:T(2,128)S(1)} %get-tuple-element.45), channel_id=1, source_target_pairs={{8,0},{16,8},{24,16},{9,1},{17,9},{25,17},{10,2},{18,10},{26,18},{... | collective-permute-start | bytes 196616 | tf_op jit(solution)/shard_map/ppermute | solution.py:19
  222.8 6.7 %collective-permute-start.13 = (f32[2,64,128]{2,0,1:T(2,128)S(1)}, f32[2,64,128]{2,0,1:T(2,128)S(1)}, u32[]{:S(2)}, u32[]{:S(2)}) collective-permute-start(f32[2,64,128]{2,0,1:T(2,128)S(1)} %get-tuple-element.44), channel_id=1, source_target_pairs={{0,8},{8,16},{16,24},{1,9},{9,17},{17,25},{2,10},{10,18},{18,26},{... | collective-permute-start | bytes 196616 | tf_op jit(solution)/shard_map/ppermute | solution.py:17
  230.4 6.2 %collective-permute-start.14 = (f32[68,2,128]{2,0,1:T(8,128)S(1)}, f32[68,2,128]{2,0,1:T(8,128)S(1)}, u32[]{:S(2)}, u32[]{:S(2)}) collective-permute-start(f32[68,2,128]{2,0,1:T(8,128)S(1)} %get-tuple-element.33), channel_id=1, source_target_pairs={{2,0},{4,2},{6,4},{3,1},{5,3},{7,5},{10,8},{12,10},{14,12},{11,9},... | collective-permute-start | bytes 208904 | tf_op jit(solution)/shard_map/ppermute | solution.py:19
  231.7 6.5 %collective-permute-start.15 = (f32[68,2,128]{2,0,1:T(8,128)S(1)}, f32[68,2,128]{2,0,1:T(8,128)S(1)}, u32[]{:S(2)}, u32[]{:S(2)}) collective-permute-start(f32[68,2,128]{2,0,1:T(8,128)S(1)} %get-tuple-element.32), channel_id=1, source_target_pairs={{0,2},{2,4},{4,6},{1,3},{3,5},{5,7},{8,10},{10,12},{12,14},{9,11},... | collective-permute-start | bytes 208904 | tf_op jit(solution)/shard_map/ppermute | solution.py:17
  245.7 10.2 %collective-permute-start.17 = (f32[68,68,2]{1,0,2:T(8,128)S(1)}, f32[68,68,2]{1,0,2:T(8,128)S(1)}, u32[]{:S(2)}, u32[]{:S(2)}) collective-permute-start(f32[68,68,2]{1,0,2:T(8,128)S(1)} %copy.121), channel_id=1, source_target_pairs={{0,1},{2,3},{4,5},{6,7},{8,9},{10,11},{12,13},{14,15},{16,17},{18,... | collective-permute-start | bytes 110984 | tf_op jit(solution)/shard_map/ppermute | solution.py:17
  249.6 8.7 %collective-permute-start.16 = (f32[68,68,2]{1,0,2:T(8,128)S(1)}, f32[68,68,2]{1,0,2:T(8,128)S(1)}, u32[]{:S(2)}, u32[]{:S(2)}) collective-permute-start(f32[68,68,2]{1,0,2:T(8,128)S(1)} %copy.119), channel_id=1, source_target_pairs={{1,0},{3,2},{5,4},{7,6},{9,8},{11,10},{13,12},{15,14},{17,16},{19,... | collective-permute-start | bytes 110984 | tf_op jit(solution)/shard_map/ppermute | solution.py:19
  331.1 20.6 %copy-start.2 = (f32[16,128]{1,0:T(8,128)S(1)}, f32[16,128]{1,0:T(8,128)}, u32[]{:S(2)}) copy-start(f32[16,128]{1,0:T(8,128)} %param.10) | copy-start | bytes 24580
  331.1 20.6 %copy-start.3 = (f32[16,128]{1,0:T(8,128)S(1)}, f32[16,128]{1,0:T(8,128)}, u32[]{:S(2)}) copy-start(f32[16,128]{1,0:T(8,128)} %param.8) | copy-start | bytes 24580
  331.1 20.6 %copy-start.4 = (f32[16,128]{1,0:T(8,128)S(1)}, f32[16,128]{1,0:T(8,128)}, u32[]{:S(2)}) copy-start(f32[16,128]{1,0:T(8,128)} %param.9) | copy-start | bytes 24580
where the time goes:
time: 354 us; the launch traced here: 352 us
  blocking collectives  151 us (43%)
  other arithmetic  91.3 us (26%)
  starting transfers between devices  44.4 us (13%)
  local copies, waits for them, and re-layouts  43.1 us (12%)
  waiting for transfers between devices  11.5 us (3%)
  between operations  10.9 us (3%)
    psum x3, blocking collectives, paired_sums(): lax.psum((jnp.sum(residual * precond), jnp.sum(image * precond)), ('gx',...  133 us
    reduce_sum x3, other arithmetic, paired_sums(): jnp.sum(image * precond)  55 us
    ppermute x9, starting transfers between devices, extended(): lax.ppermute(tail, axis, [(i, (i + 1) % count) for i in range(ends)])  32.7 us
    psum x1, blocking collectives, per_device(): whole_strip = lax.psum(fault_term, 'gy')  17.9 us
    slice x6, local copies, waits for them, and re-layouts, extended(): head = lax.slice_in_dim(cells, 0, width, axis=dim)  16.8 us
    concatenate x9, other arithmetic, extended(): jnp.concatenate([lax.ppermute(tail, axis, [(i, (i + 1) % count) for i in...  16 us
    ppermute x9, starting transfers between devices, extended(): lax.ppermute(head, axis, [((i + 1) % count, i) for i in range(ends)])  11.6 us
    mul x2, other arithmetic, per_device(): precond = inverse * residual  9.98 us
  transfers between devices with their start and end apart: 18, of which 12 were waited for; matrix products, arithmetic and copies ran while one was open for 8% of the time, Pallas kernels for 0%

commit v1 on v0

v1 whole, which is shorter than its diff:
```python
import jax
import jax.numpy as jnp
from jax import lax
from jax.experimental import pallas as pl
from jax.experimental.pallas import tpu as pltpu
from jax.sharding import PartitionSpec as P

MESH = pl.DeviceIdType.MESH
AXES = ("gx", "gy", "gz")
PAD = 8
CHUNK = 8


def total(values):
    return jnp.sum(values.reshape(-1, 8, values.shape[-1]), axis=0)


def solve(t0, s):
    t1 = t0 - s[0]
    t2 = t1 - s[1]
    tiny = 1e-7
    p0 = s[0]
    l10 = s[1] / p0
    l20 = s[2] / p0
    p1 = s[2] - l10 * s[1]
    q = s[3] - l20 * s[1]
    ok1 = p1 > tiny * s[2]
    i1 = jnp.where(ok1, 1.0 / jnp.where(ok1, p1, 1.0), 0.0)
    l21 = q * i1
    p2 = s[4] - l20 * s[2] - l21 * q
    ok2 = ok1 & (p2 > tiny * s[4])
    i2 = jnp.where(ok2, 1.0 / jnp.where(ok2, p2, 1.0), 0.0)
    y1 = t1 - l10 * t0
    y2 = t2 - l20 * t0 - l21 * y1
    c2 = y2 * i2
    c1 = y1 * i1 - l21 * c2
    c0 = t0 / p0 - l10 * c1 - l20 * c2
    return c0, c1, c2


def make_kernel(sizes):
    ngx, ngy, ngz = sizes
    count = ngx * ngy * ngz

    def kernel(load, stiff, pre_ref, state_ref, norm_ref, out, slip,
               b, d, u0, u1, u2, obuf, ysend, yrecv, zsend, zrecv, fsend, frecv, red,
               in_sem, out_sem, send_sem, recv_sem, fs_sem, fr_sem, rs_sem, rr_sem):
        nx, ny, nz = b.shape
        us = (u0, u1, u2)
        ix, iy, iz = (lax.axis_index(a) for a in AXES)
        me = (ix * ngy + iy) * ngz + iz
        spots = (ix, iy, iz)

        def other(step):
            who = lax.rem(me + step, count)
            return (who // (ngy * ngz), lax.rem(who // ngz, ngy), lax.rem(who, ngz))

        chunks = nx // CHUNK
        order = [0, chunks - 1] + list(range(1, chunks - 1))
        copies = {}
        for c in order:
            part = pl.ds(c * CHUNK, CHUNK)
            copies[c] = (
                pltpu.make_async_copy(load.at[part], b.at[part], in_sem.at[0, c]),
                pltpu.make_async_copy(stiff.at[part], d.at[part], in_sem.at[1, c]),
            )
            for one in copies[c]:
                one.start()

        barrier = pltpu.get_barrier_semaphore()

        @pl.loop(1, count)
        def _(step):
            pl.semaphore_signal(barrier, inc=1, device_id=other(step), device_id_type=MESH)

        zero_plane = jnp.zeros((2, ny, nz), jnp.float32)
        zero_rows = jnp.zeros((nx, 2, nz), jnp.float32)
        for k in range(3):
            @pl.when(ix == 0)
            def _():
                us[k][0:2, PAD:PAD + ny, :] = zero_plane
            @pl.when(ix == ngx - 1)
            def _():
                us[k][nx + 2:nx + 4, PAD:PAD + ny, :] = zero_plane
            @pl.when(iy == 0)
            def _():
                yrecv[k, 0] = zero_rows
            @pl.when(iy == ngy - 1)
            def _():
                yrecv[k, 1] = zero_rows

        lane = lax.broadcasted_iota(jnp.int32, (ny, nz), 1)
        first = iz == 0
        send_base = jnp.where(first, 2, 0)
        recv_base = jnp.where(first, nz, 2 * nz - 2)

        def place(field, x, value, k, pack):
            us[k][x + 2, PAD:PAD + ny, :] = value
            ysend[k, 0, x] = value[0:2]
            ysend[k, 1, x] = value[ny - 2:ny]
            moved = pltpu.roll(value, lax.rem(2 * x + send_base, nz), 1)
            return jnp.where((lane >> 1) == x, moved, pack)

        def xcopy(k, side):
            u = us[k]
            if side == 0:
                src, dst, to = u.at[2:4, PAD:PAD + ny], u.at[nx + 2:nx + 4, PAD:PAD + ny], ix - 1
            else:
                src, dst, to = u.at[nx:nx + 2, PAD:PAD + ny], u.at[0:2, PAD:PAD + ny], ix + 1
            return pltpu.make_async_remote_copy(
                src, dst, send_sem.at[k, side], recv_sem.at[k, side],
                device_id=(to, iy, iz), device_id_type=MESH)

        def ycopy(k, side):
            to = iy - 1 if side == 0 else iy + 1
            return pltpu.make_async_remote_copy(
                ysend.at[k, side], yrecv.at[k, 1 - side], send_sem.at[k, 2 + side],
                recv_sem.at[k, 2 + side], device_id=(ix, to, iz), device_id_type=MESH)

        def zcopy(k):
            return pltpu.make_async_remote_copy(
                zsend.at[k], zrecv.at[k], send_sem.at[k, 4], recv_sem.at[k, 4],
                device_id=(ix, iy, 1 - iz), device_id_type=MESH)

        def sending(spot, size, side):
            return spot > 0 if side == 0 else spot < size - 1

        def receiving(spot, size, side):
            return spot < size - 1 if side == 0 else spot > 0

        def sides(k):
            return (1,) if k == 2 else (0, 1)

        def each(make, k, spot, size, test, act):
            for side in sides(k):
                @pl.when(test(spot, size, side))
                def _():
                    act(make(k, side))

        def start_x(k):
            each(xcopy, k, ix, ngx, sending, lambda c: c.start())

        def start_yz(k):
            each(ycopy, k, iy, ngy, sending, lambda c: c.start())
            zcopy(k).start()

        def scale(x, carry):
            t0, pack = carry
            inv = 1.0 / (7.5 + d[x])
            d[x] = inv
            rhs = b[x]
            value = inv * rhs
            return t0 + total(value * rhs), place(u0, x, value, 0, pack)

        carry = (jnp.zeros((8, nz), jnp.float32), jnp.zeros((ny, nz), jnp.float32))
        for n, c in enumerate(order):
            for one in copies[c]:
                one.wait()
            carry = lax.fori_loop(c * CHUNK, (c + 1) * CHUNK, scale, carry)
            if n == 1:
                pl.semaphore_wait(barrier, count - 1)
                start_x(0)
        t0, pack = carry
        zsend[0] = pack
        start_yz(0)

        def wait_y(k):
            each(ycopy, k, iy, ngy, receiving, lambda c: c.wait_recv())

        def wait_x(k):
            each(xcopy, k, ix, ngx, receiving, lambda c: c.wait_recv())

        def ends(k, x, value):
            got = pltpu.roll(zrecv[k], lax.rem(recv_base - 2 * x, nz), 1)
            nothing = jnp.zeros_like(got)
            low = jnp.where(first, nothing, got)
            high = jnp.where(first, got, nothing)
            return (
                pltpu.roll(jnp.where(lane >= nz - 1, low, value), 1, 1),
                pltpu.roll(jnp.where(lane >= nz - 2, low, value), 2, 1),
                pltpu.roll(jnp.where(lane < 1, high, value), nz - 1, 1),
                pltpu.roll(jnp.where(lane < 2, high, value), nz - 2, 1),
            )

        def near(k, x):
            u = us[k]
            u[x + 2, PAD - 2:PAD, :] = yrecv[k, 0, x]
            u[x + 2, PAD + ny:PAD + ny + 2, :] = yrecv[k, 1, x]
            value = u[x + 2, PAD:PAD + ny, :]
            low1, low2, high1, high2 = ends(k, x, value)
            one = (u[x + 1, PAD:PAD + ny, :] + u[x + 3, PAD:PAD + ny, :]
                   + u[x + 2, PAD - 1:PAD - 1 + ny, :] + u[x + 2, PAD + 1:PAD + 1 + ny, :]
                   + low1 + high1)
            two = (u[x, PAD:PAD + ny, :] + u[x + 4, PAD:PAD + ny, :]
                   + u[x + 2, PAD - 2:PAD - 2 + ny, :] + u[x + 2, PAD + 2:PAD + 2 + ny, :]
                   + low2 + high2)
            return value, (16.0 * one - two) * (1.0 / 12.0)

        def half_near(k, x):
            u = us[k]
            u[x + 2, PAD - 2:PAD, :] = yrecv[k, 0, x]
            value = u[x + 2, PAD:PAD + ny, :]
            low1, low2, _, _ = ends(k, x, value)
            one = (u[x + 1, PAD:PAD + ny, :] + u[x + 2, PAD - 1:PAD - 1 + ny, :]
                   + low1)
            two = (u[x, PAD:PAD + ny, :] + u[x + 2, PAD - 2:PAD - 2 + ny, :]
                   + low2)
            return value, (16.0 * one - two) * (1.0 / 6.0)

        zero = jnp.zeros((8, nz), jnp.float32)

        def run(step, k, carry, low_edge, high_edge):
            carry = lax.fori_loop(2, nx - 2 if high_edge else nx, step, carry)
            wait_x(k)
            carry = lax.fori_loop(0, 2, step, carry)
            if high_edge:
                carry = lax.fori_loop(nx - 2, nx, step, carry)
            return carry

        def advance(k):
            def step(x, carry):
                even, odd, pack = carry
                value, w = near(k, x)
                fresh = d[x] * w
                even = even + total(value * (b[x] - w))
                odd = odd + total((value - fresh) * w)
                b[x] = w
                return even, odd, place(None, x, fresh, k + 1, pack)

            zcopy(k).wait_recv()
            wait_y(k)
            even, odd, pack = run(step, k, (zero, zero, jnp.zeros((ny, nz), jnp.float32)), True, True)
            start_x(k + 1)
            zsend[k + 1] = pack
            start_yz(k + 1)
            return even, odd

        s0, s1 = advance(0)
        s2, s3 = advance(1)

        owned = nx // ngy
        below = iy == ngy // 2 - 1
        above = iy == ngy // 2

        def fault_copy(which, to):
            return pltpu.make_async_remote_copy(
                fsend.at[:, pl.ds(to * owned, owned), :], frecv.at[which], fs_sem.at[to], fr_sem.at[which],
                device_id=(ix, to, iz), device_id_type=MESH)

        @pl.when(below | above)
        def _():
            edge = jnp.where(below, 1, 0)
            far = jnp.where(below, 1.0 / 24.0, 27.0 / 24.0)
            close = jnp.where(below, -27.0 / 24.0, -1.0 / 24.0)

            @pl.loop(0, nx)
            def _(x):
                for j in range(3):
                    rows = ysend[j, edge, x]
                    fsend[j, pl.ds(x, 1), :] = far * rows[0:1] + close * rows[1:2]

        for which, owner in enumerate((ngy // 2 - 1, ngy // 2)):
            @pl.when(iy == owner)
            def _():
                for to in range(ngy):
                    if to != owner:
                        fault_copy(which, to).start()
                frecv[which] = fsend[:, owner * owned:(owner + 1) * owned, :]

        def last(x, s4):
            value, w = half_near(2, x)
            return s4 + total(value * (b[x] - w))

        zcopy(2).wait_recv()
        wait_y(2)
        s4 = run(last, 2, zero, True, False)

        slot = lax.broadcasted_iota(jnp.int32, (1, nz), 1)
        row = jnp.zeros((1, nz), jnp.float32)
        for j, part in enumerate((t0, s0, s1, s2, s3, s4)):
            whole = jnp.sum(jnp.sum(part, axis=1, keepdims=True), axis=0, keepdims=True)
            row = row + jnp.where(slot == j, whole, 0.0)
        red[me] = row

        def sum_copy(step):
            return pltpu.make_async_remote_copy(
                red.at[me], red.at[me], rs_sem.at[step], rr_sem.at[me],
                device_id=other(step), device_id_type=MESH)

        @pl.loop(1, count)
        def _(step):
            sum_copy(step).start()

        @pl.loop(1, count)
        def _(step):
            who = lax.rem(me + step, count)
            pltpu.make_async_remote_copy(
                red.at[who], red.at[who], rs_sem.at[step], rr_sem.at[who],
                device_id=other(step), device_id_type=MESH).wait_recv()

        sums = jnp.sum(red[...], axis=0)
        parts = [jnp.sum(jnp.where(slot == j, sums, 0.0), axis=1, keepdims=True) for j in range(6)]
        coefs = [jnp.broadcast_to(c, (1, nz)) for c in solve(parts[0], parts[1:])]

        def out_copy(c):
            part = pl.ds(c * CHUNK, CHUNK)
            return pltpu.make_async_copy(obuf.at[part], out.at[part], out_sem.at[c])

        def blend(x, carry):
            mid = slice(PAD, PAD + ny)
            obuf[x] = (coefs[0] * u0[x + 2, mid, :] + coefs[1] * u1[x + 2, mid, :]
                       + coefs[2] * u2[x + 2, mid, :])
            return carry

        for c in range(chunks):
            lax.fori_loop(c * CHUNK, (c + 1) * CHUNK, blend, 0)
            out_copy(c).start()

        for which, owner in enumerate((ngy // 2 - 1, ngy // 2)):
            @pl.when(iy != owner)
            def _():
                fault_copy(which, owner).wait_recv()
        traction = sum(coefs[j] * (frecv[0, j] + frecv[1, j]) for j in range(3))
        arg = (pre_ref[...] + 2.0 * traction) / norm_ref[...]
        half = jnp.float32(-0.6931471805599453)
        small = arg * (1.0 + arg * arg * (1.0 / 6.0) * (1.0 + arg * arg * 0.05))
        sinh = jnp.where(jnp.abs(arg) < 0.25, small, jnp.exp(arg + half) - jnp.exp(half - arg))
        slip[...] = jnp.exp(-state_ref[...]) * sinh

        for k in range(3):
            each(xcopy, k, ix, ngx, sending, lambda c: c.wait_send())
            each(ycopy, k, iy, ngy, sending, lambda c: c.wait_send())
            zcopy(k).wait_send()
        for which, owner in enumerate((ngy // 2 - 1, ngy // 2)):
            @pl.when(iy == owner)
            def _():
                for to in range(ngy):
                    if to != owner:
                        fault_copy(which, to).wait_send()

        @pl.loop(1, count)
        def _(step):
            sum_copy(step).wait_send()

        for c in range(chunks):
            out_copy(c).wait()

    return kernel


def solution(mesh):
    sizes = tuple(mesh.shape[a] for a in AXES)
    assert sizes[1] % 2 == 0 and sizes[2] == 2

    def per_device(load, stiffness, prestress, state_var, normal_a):
        nx, ny, nz = load.shape
        assert 2 * nx <= nz and nx % CHUNK == 0
        f32 = jnp.float32
        count = sizes[0] * sizes[1] * sizes[2]
        padded = (nx + 4, ny + 2 * PAD, nz)
        vmem = pl.BlockSpec(memory_space=pltpu.VMEM)
        hbm = pl.BlockSpec(memory_space=pl.ANY)
        dma = pltpu.SemaphoreType.DMA
        return pl.pallas_call(
            make_kernel(sizes),
            out_shape=(
                jax.ShapeDtypeStruct(load.shape, f32),
                jax.ShapeDtypeStruct(prestress.shape, f32),
            ),
            in_specs=[hbm, hbm, vmem, vmem, vmem],
            out_specs=(hbm, vmem),
            scratch_shapes=[
                pltpu.VMEM((nx, ny, nz), f32),
                pltpu.VMEM((nx, ny, nz), f32),
                pltpu.VMEM(padded, f32),
                pltpu.VMEM(padded, f32),
                pltpu.VMEM(padded, f32),
                pltpu.VMEM((nx, ny, nz), f32),
                pltpu.VMEM((3, 2, nx, 2, nz), f32),
                pltpu.VMEM((3, 2, nx, 2, nz), f32),
                pltpu.VMEM((3, ny, nz), f32),
                pltpu.VMEM((3, ny, nz), f32),
                pltpu.VMEM((3, nx, nz), f32),
                pltpu.VMEM((2, 3, nx // sizes[1], nz), f32),
                pltpu.VMEM((count, 1, nz), f32),
                dma((2, nx // CHUNK)),
                dma((nx // CHUNK,)),
                dma((3, 5)),
                dma((3, 5)),
                dma((sizes[1],)),
                dma((2,)),
                dma((count,)),
                dma((count,)),
            ],
            compiler_params=pltpu.CompilerParams(collective_id=0, has_side_effects=True),
        )(load, stiffness, prestress, state_var, normal_a)

    placed = (
        P("gx", "gy", "gz"),
        P("gx", "gy", "gz"),
        P(("gx", "gy"), "gz"),
        P(("gx", "gy"), "gz"),
        P(("gx", "gy"), "gz"),
    )
    return jax.shard_map(
        per_device,
        mesh=mesh,
        in_specs=placed,
        out_specs=(P("gx", "gy", "gz"), P(("gx", "gy"), "gz")),
        check_vma=False,
    )
```

time: 354 us -> 76.7 us (0.22)
  blocking collectives: 151 us -> 0 us
  other arithmetic: 91.3 us -> 0 us
  Pallas kernels: 0 us -> 72.1 us
  starting transfers between devices: 44.4 us -> 0 us
  local copies, waits for them, and re-layouts: 43.1 us -> 3.77 us
  waiting for transfers between devices: 11.5 us -> 0 us
  between operations: 10.9 us -> 0.65 us
    psum x4 -> x0, blocking collectives: 151 us -> none  [the longest x3 133 us: paired_sums(): lax.psum((jnp.sum(residual * precond), jnp.sum(image * precond)), ('gx',...]
    pallas_call x0 -> x1, Pallas kernels: none -> 72.1 us  [per_device(): pl.pallas_call(make_kernel(sizes), out_shape=(jax.ShapeDtypeStruct(load.s...]
    reduce_sum x5 -> x0, other arithmetic: 61.7 us -> none  [the longest x3 55 us: paired_sums(): jnp.sum(image * precond)]
    ppermute x18 -> x0, starting transfers between devices: 44.4 us -> none  [the longest x9 32.7 us: extended(): lax.ppermute(tail, axis, [(i, (i + 1) % count) for i in range(ends)])]
    slice x13 -> x0, local copies, waits for them, and re-layouts: 24.8 us -> none  [the longest x6 16.8 us: extended(): head = lax.slice_in_dim(cells, 0, width, axis=dim)]
    concatenate x9 -> x0, other arithmetic: 16 us -> none  [extended(): jnp.concatenate([lax.ppermute(tail, axis, [(i, (i + 1) % count) for i in...]
    ppermute x6 -> x0, local copies, waits for them, and re-layouts: 14.5 us -> none  [the longest x3 7.28 us: extended(): lax.ppermute(head, axis, [((i + 1) % count, i) for i in range(ends)])]
    ppermute x18 -> x0, waiting for transfers between devices: 11.5 us -> none  [the longest x9 9.47 us: extended(): lax.ppermute(tail, axis, [(i, (i + 1) % count) for i in range(ends)])]
  transfers between devices with their start and end apart: 18 -> 0, of which waited for: 12 -> 0; matrix products, arithmetic and copies ran while one was open for 8% -> 0% of each run, Pallas kernels for 0% -> 0%
where the time goes in v1:
time: 76.7 us; the launch traced here: 76.5 us
  Pallas kernels  72.1 us (94%)
  local copies, waits for them, and re-layouts  3.77 us (5%)
    pallas_call x1, Pallas kernels, per_device(): pl.pallas_call(make_kernel(sizes), out_shape=(jax.ShapeDtypeStruct(load.s...  72.1 us
    unnamed x4, local copies, waits for them, and re-layouts  3.77 us

profile of v1, /device:TPU:0, one launch (start us, length us, event | category | flops | bytes accessed | tf_op | source)
XLA Modules:
  0.0 76.5 jit_solution(2259520333801237407)
XLA Ops:
  0.6 72.1 %shard_map.68 = (f32[64,64,128]{2,1,0:T(8,128)}, f32[16,128]{1,0:T(8,128)}) custom-call(f32[64,64,128]{2,1,0:T(8,128)} %load.1, f32[64,64,128]{2,1,0:T(8,128)} %stiff.1, f32[16,128]{1,0:T(8,128)} %pre_ref.1, f32[16,128]{1,0:T(8,128)} %state_ref.1, f32[16,128]{1,0:T(8,128)} %norm_ref.1), custom_call_target="tpu_custom_call" | custom-call | tf_op jit(solution)/shard_map/pallas_call | solution.py:364
  72.7 0.0 copy-start
  72.7 3.2 %copy.9 = f32[64,64,128]{2,1,0:T(8,128)} copy(f32[64,64,128]{2,1,0:T(8,128)} %get-tuple-element.4) | data formatting | bytes 4194304
  75.9 0.0 copy-done
  75.9 0.6 copy.10
Async XLA Ops:
  72.7 3.2 %copy-start = (f32[16,128]{1,0:T(8,128)S(1)}, f32[16,128]{1,0:T(8,128)}, u32[]{:S(2)}) copy-start(f32[16,128]{1,0:T(8,128)} %get-tuple-element.5) | copy-start | bytes 24580

commit v2 on v1

--- a/solution.py
+++ b/solution.py
@@ -9,6 +9,7 @@
 AXES = ("gx", "gy", "gz")
 PAD = 8
 CHUNK = 8
+GROUP = 2
 
 
 def total(values):
@@ -38,13 +39,25 @@
     return c0, c1, c2
 
 
+def parts_of(nx):
+    inner = nx - 4
+    runs = max(n for n in range(1, 7) if inner % (GROUP * n) == 0)
+    size = inner // runs
+    return [(0, 2), (nx - 2, 2)] + [(2 + n * size, size) for n in range(runs)]
+
+
+def halves(values):
+    high = values.astype(jnp.bfloat16)
+    return high, (values - high.astype(jnp.float32)).astype(jnp.bfloat16)
+
+
 def make_kernel(sizes):
     ngx, ngy, ngz = sizes
     count = ngx * ngy * ngz
 
     def kernel(load, stiff, pre_ref, state_ref, norm_ref, out, slip,
-               b, d, u0, u1, u2, obuf, ysend, yrecv, zsend, zrecv, fsend, frecv, red,
-               in_sem, out_sem, send_sem, recv_sem, fs_sem, fr_sem, rs_sem, rr_sem):
+               b, d, u0, u1, u2, obuf, ysend, yrecv, zrecv, band, fsend, frecv, red,
+               in_sem, out_sem, send_sem, recv_sem, zs_sem, zr_sem, fs_sem, fr_sem, rs_sem, rr_sem):
         nx, ny, nz = b.shape
         us = (u0, u1, u2)
         ix, iy, iz = (lax.axis_index(a) for a in AXES)
@@ -55,16 +68,15 @@
             who = lax.rem(me + step, count)
             return (who // (ngy * ngz), lax.rem(who // ngz, ngy), lax.rem(who, ngz))
 
-        chunks = nx // CHUNK
-        order = [0, chunks - 1] + list(range(1, chunks - 1))
-        copies = {}
-        for c in order:
-            part = pl.ds(c * CHUNK, CHUNK)
-            copies[c] = (
-                pltpu.make_async_copy(load.at[part], b.at[part], in_sem.at[0, c]),
-                pltpu.make_async_copy(stiff.at[part], d.at[part], in_sem.at[1, c]),
-            )
-            for one in copies[c]:
+        parts = parts_of(nx)
+        copies = []
+        for n, (at, size) in enumerate(parts):
+            part = pl.ds(at, size)
+            copies.append((
+                pltpu.make_async_copy(load.at[part], b.at[part], in_sem.at[0, n]),
+                pltpu.make_async_copy(stiff.at[part], d.at[part], in_sem.at[1, n]),
+            ))
+            for one in copies[n]:
                 one.start()
 
         barrier = pltpu.get_barrier_semaphore()
@@ -89,17 +101,20 @@
             def _():
                 yrecv[k, 1] = zero_rows
 
-        lane = lax.broadcasted_iota(jnp.int32, (ny, nz), 1)
-        first = iz == 0
-        send_base = jnp.where(first, 2, 0)
-        recv_base = jnp.where(first, nz, 2 * nz - 2)
-
-        def place(field, x, value, k, pack):
+        row = lax.broadcasted_iota(jnp.int32, (nz, nz), 0)
+        col = lax.broadcasted_iota(jnp.int32, (nz, nz), 1)
+        far = row + jnp.where(iz == 0, nz, -nz)
+        for n, at in enumerate((row, far, row, far)):
+            gap = col - at
+            full = jnp.where(jnp.abs(gap) == 1, 16.0, 0.0) - jnp.where(jnp.abs(gap) == 2, 1.0, 0.0)
+            half = jnp.where(gap == 1, 16.0, 0.0) - jnp.where(gap == 2, 1.0, 0.0)
+            band[0, n * nz:(n + 1) * nz, :] = full.astype(jnp.bfloat16)
+            band[1, n * nz:(n + 1) * nz, :] = half.astype(jnp.bfloat16)
+
+        def place(x, value, k):
             us[k][x + 2, PAD:PAD + ny, :] = value
             ysend[k, 0, x] = value[0:2]
             ysend[k, 1, x] = value[ny - 2:ny]
-            moved = pltpu.roll(value, lax.rem(2 * x + send_base, nz), 1)
-            return jnp.where((lane >> 1) == x, moved, pack)
 
         def xcopy(k, side):
             u = us[k]
@@ -117,9 +132,10 @@
                 ysend.at[k, side], yrecv.at[k, 1 - side], send_sem.at[k, 2 + side],
                 recv_sem.at[k, 2 + side], device_id=(ix, to, iz), device_id_type=MESH)
 
-        def zcopy(k):
+        def zcopy(k, at, size, n):
             return pltpu.make_async_remote_copy(
-                zsend.at[k], zrecv.at[k], send_sem.at[k, 4], recv_sem.at[k, 4],
+                us[k].at[pl.ds(at + 2, size), PAD:PAD + ny], zrecv.at[k, pl.ds(at, size)],
+                zs_sem.at[k, n], zr_sem.at[k, n],
                 device_id=(ix, iy, 1 - iz), device_id_type=MESH)
 
         def sending(spot, size, side):
@@ -140,29 +156,29 @@
         def start_x(k):
             each(xcopy, k, ix, ngx, sending, lambda c: c.start())
 
-        def start_yz(k):
+        def start_y(k):
             each(ycopy, k, iy, ngy, sending, lambda c: c.start())
-            zcopy(k).start()
-
-        def scale(x, carry):
-            t0, pack = carry
+
+        def scale(x, t0):
             inv = 1.0 / (7.5 + d[x])
             d[x] = inv
             rhs = b[x]
             value = inv * rhs
-            return t0 + total(value * rhs), place(u0, x, value, 0, pack)
-
-        carry = (jnp.zeros((8, nz), jnp.float32), jnp.zeros((ny, nz), jnp.float32))
-        for n, c in enumerate(order):
-            for one in copies[c]:
+            place(x, value, 0)
+            return t0 + total(value * rhs)
+
+        t0 = jnp.zeros((8, nz), jnp.float32)
+        for n, (at, size) in enumerate(parts):
+            for one in copies[n]:
                 one.wait()
-            carry = lax.fori_loop(c * CHUNK, (c + 1) * CHUNK, scale, carry)
+            t0 = lax.fori_loop(at, at + size, scale, t0)
             if n == 1:
                 pl.semaphore_wait(barrier, count - 1)
                 start_x(0)
-        t0, pack = carry
-        zsend[0] = pack
-        start_yz(0)
+                zcopy(0, *parts[0], 0).start()
+            if n >= 1:
+                zcopy(0, at, size, n).start()
+        start_y(0)
 
         def wait_y(k):
             each(ycopy, k, iy, ngy, receiving, lambda c: c.wait_recv())
@@ -170,69 +186,71 @@
         def wait_x(k):
             each(xcopy, k, ix, ngx, receiving, lambda c: c.wait_recv())
 
-        def ends(k, x, value):
-            got = pltpu.roll(zrecv[k], lax.rem(recv_base - 2 * x, nz), 1)
-            nothing = jnp.zeros_like(got)
-            low = jnp.where(first, nothing, got)
-            high = jnp.where(first, got, nothing)
-            return (
-                pltpu.roll(jnp.where(lane >= nz - 1, low, value), 1, 1),
-                pltpu.roll(jnp.where(lane >= nz - 2, low, value), 2, 1),
-                pltpu.roll(jnp.where(lane < 1, high, value), nz - 1, 1),
-                pltpu.roll(jnp.where(lane < 2, high, value), nz - 2, 1),
-            )
-
-        def near(k, x):
+        def along_z(k, x, which):
+            own = us[k][pl.ds(x + 2, GROUP), PAD:PAD + ny, :].reshape(GROUP * ny, nz)
+            next_to = zrecv[k, pl.ds(x, GROUP)].reshape(GROUP * ny, nz)
+            own_high, own_low = halves(own)
+            next_high, next_low = halves(next_to)
+            lhs = jnp.concatenate([own_high, next_high, own_low, next_low], axis=1)
+            return jnp.dot(lhs, band[which], preferred_element_type=jnp.float32)
+
+        def near(k, x, z_term):
             u = us[k]
             u[x + 2, PAD - 2:PAD, :] = yrecv[k, 0, x]
             u[x + 2, PAD + ny:PAD + ny + 2, :] = yrecv[k, 1, x]
-            value = u[x + 2, PAD:PAD + ny, :]
-            low1, low2, high1, high2 = ends(k, x, value)
             one = (u[x + 1, PAD:PAD + ny, :] + u[x + 3, PAD:PAD + ny, :]
-                   + u[x + 2, PAD - 1:PAD - 1 + ny, :] + u[x + 2, PAD + 1:PAD + 1 + ny, :]
-                   + low1 + high1)
+                   + u[x + 2, PAD - 1:PAD - 1 + ny, :] + u[x + 2, PAD + 1:PAD + 1 + ny, :])
             two = (u[x, PAD:PAD + ny, :] + u[x + 4, PAD:PAD + ny, :]
-                   + u[x + 2, PAD - 2:PAD - 2 + ny, :] + u[x + 2, PAD + 2:PAD + 2 + ny, :]
-                   + low2 + high2)
-            return value, (16.0 * one - two) * (1.0 / 12.0)
-
-        def half_near(k, x):
+                   + u[x + 2, PAD - 2:PAD - 2 + ny, :] + u[x + 2, PAD + 2:PAD + 2 + ny, :])
+            return (16.0 * one - two + z_term) * (1.0 / 12.0)
+
+        def half_near(k, x, z_term):
             u = us[k]
             u[x + 2, PAD - 2:PAD, :] = yrecv[k, 0, x]
-            value = u[x + 2, PAD:PAD + ny, :]
-            low1, low2, _, _ = ends(k, x, value)
-            one = (u[x + 1, PAD:PAD + ny, :] + u[x + 2, PAD - 1:PAD - 1 + ny, :]
-                   + low1)
-            two = (u[x, PAD:PAD + ny, :] + u[x + 2, PAD - 2:PAD - 2 + ny, :]
-                   + low2)
-            return value, (16.0 * one - two) * (1.0 / 6.0)
+            one = u[x + 1, PAD:PAD + ny, :] + u[x + 2, PAD - 1:PAD - 1 + ny, :]
+            two = u[x, PAD:PAD + ny, :] + u[x + 2, PAD - 2:PAD - 2 + ny, :]
+            return (16.0 * one - two + z_term) * (1.0 / 6.0)
 
         zero = jnp.zeros((8, nz), jnp.float32)
 
-        def run(step, k, carry, low_edge, high_edge):
-            carry = lax.fori_loop(2, nx - 2 if high_edge else nx, step, carry)
+        def run(plane, k, carry, which, done):
+            def group(at, n, carry):
+                x = at + n * GROUP
+                z_terms = along_z(k, x, which)
+                for g in range(GROUP):
+                    carry = plane(x + g, z_terms[g * ny:(g + 1) * ny], carry)
+                return carry
+
+            def part(at, size, n, carry):
+                zcopy(k, at, size, n).wait_recv()
+                carry = lax.fori_loop(0, size // GROUP, lambda i, c: group(at, i, c), carry)
+                done(at, size, n)
+                return carry
+
+            first_at, size = parts[2]
+            carry = lax.fori_loop(
+                0, len(parts) - 2, lambda n, c: part(first_at + n * size, size, n + 2, c), carry)
             wait_x(k)
-            carry = lax.fori_loop(0, 2, step, carry)
-            if high_edge:
-                carry = lax.fori_loop(nx - 2, nx, step, carry)
+            for n in range(2):
+                carry = part(*parts[n], n, carry)
             return carry
 
         def advance(k):
-            def step(x, carry):
-                even, odd, pack = carry
-                value, w = near(k, x)
+            def plane(x, z_term, carry):
+                even, odd = carry
+                value = us[k][x + 2, PAD:PAD + ny, :]
+                w = near(k, x, z_term)
                 fresh = d[x] * w
                 even = even + total(value * (b[x] - w))
                 odd = odd + total((value - fresh) * w)
                 b[x] = w
-                return even, odd, place(None, x, fresh, k + 1, pack)
-
-            zcopy(k).wait_recv()
+                place(x, fresh, k + 1)
+                return even, odd
+
             wait_y(k)
-            even, odd, pack = run(step, k, (zero, zero, jnp.zeros((ny, nz), jnp.float32)), True, True)
+            even, odd = run(plane, k, (zero, zero), 0, lambda *p: zcopy(k + 1, *p).start())
             start_x(k + 1)
-            zsend[k + 1] = pack
-            start_yz(k + 1)
+            start_y(k + 1)
             return even, odd
 
         s0, s1 = advance(0)
@@ -250,14 +268,14 @@
         @pl.when(below | above)
         def _():
             edge = jnp.where(below, 1, 0)
-            far = jnp.where(below, 1.0 / 24.0, 27.0 / 24.0)
+            front = jnp.where(below, 1.0 / 24.0, 27.0 / 24.0)
             close = jnp.where(below, -27.0 / 24.0, -1.0 / 24.0)
 
             @pl.loop(0, nx)
             def _(x):
                 for j in range(3):
                     rows = ysend[j, edge, x]
-                    fsend[j, pl.ds(x, 1), :] = far * rows[0:1] + close * rows[1:2]
+                    fsend[j, pl.ds(x, 1), :] = front * rows[0:1] + close * rows[1:2]
 
         for which, owner in enumerate((ngy // 2 - 1, ngy // 2)):
             @pl.when(iy == owner)
@@ -267,20 +285,19 @@
                         fault_copy(which, to).start()
                 frecv[which] = fsend[:, owner * owned:(owner + 1) * owned, :]
 
-        def last(x, s4):
-            value, w = half_near(2, x)
-            return s4 + total(value * (b[x] - w))
-
-        zcopy(2).wait_recv()
+        def last(x, z_term, s4):
+            value = us[2][x + 2, PAD:PAD + ny, :]
+            return s4 + total(value * (b[x] - half_near(2, x, z_term)))
+
         wait_y(2)
-        s4 = run(last, 2, zero, True, False)
+        s4 = run(last, 2, zero, 1, lambda *p: None)
 
         slot = lax.broadcasted_iota(jnp.int32, (1, nz), 1)
-        row = jnp.zeros((1, nz), jnp.float32)
+        sent = jnp.zeros((1, nz), jnp.float32)
         for j, part in enumerate((t0, s0, s1, s2, s3, s4)):
             whole = jnp.sum(jnp.sum(part, axis=1, keepdims=True), axis=0, keepdims=True)
-            row = row + jnp.where(slot == j, whole, 0.0)
-        red[me] = row
+            sent = sent + jnp.where(slot == j, whole, 0.0)
+        red[me] = sent
 
         def sum_copy(step):
             return pltpu.make_async_remote_copy(
@@ -299,8 +316,8 @@
                 device_id=other(step), device_id_type=MESH).wait_recv()
 
         sums = jnp.sum(red[...], axis=0)
-        parts = [jnp.sum(jnp.where(slot == j, sums, 0.0), axis=1, keepdims=True) for j in range(6)]
-        coefs = [jnp.broadcast_to(c, (1, nz)) for c in solve(parts[0], parts[1:])]
+        sums = [jnp.sum(jnp.where(slot == j, sums, 0.0), axis=1, keepdims=True) for j in range(6)]
+        coefs = [jnp.broadcast_to(c, (1, nz)) for c in solve(sums[0], sums[1:])]
 
         def out_copy(c):
             part = pl.ds(c * CHUNK, CHUNK)
@@ -312,7 +329,7 @@
                        + coefs[2] * u2[x + 2, mid, :])
             return carry
 
-        for c in range(chunks):
+        for c in range(nx // CHUNK):
             lax.fori_loop(c * CHUNK, (c + 1) * CHUNK, blend, 0)
             out_copy(c).start()
 
@@ -330,7 +347,8 @@
         for k in range(3):
             each(xcopy, k, ix, ngx, sending, lambda c: c.wait_send())
             each(ycopy, k, iy, ngy, sending, lambda c: c.wait_send())
-            zcopy(k).wait_send()
+            for n, (at, size) in enumerate(parts):
+                zcopy(k, at, size, n).wait_send()
         for which, owner in enumerate((ngy // 2 - 1, ngy // 2)):
             @pl.when(iy == owner)
             def _():
@@ -342,7 +360,7 @@
         def _(step):
             sum_copy(step).wait_send()
 
-        for c in range(chunks):
+        for c in range(nx // CHUNK):
             out_copy(c).wait()
 
     return kernel
@@ -354,7 +372,8 @@
 
     def per_device(load, stiffness, prestress, state_var, normal_a):
         nx, ny, nz = load.shape
-        assert 2 * nx <= nz and nx % CHUNK == 0
+        assert nx % CHUNK == 0
+        runs = len(parts_of(nx))
         f32 = jnp.float32
         count = sizes[0] * sizes[1] * sizes[2]
         padded = (nx + 4, ny + 2 * PAD, nz)
@@ -378,15 +397,17 @@
                 pltpu.VMEM((nx, ny, nz), f32),
                 pltpu.VMEM((3, 2, nx, 2, nz), f32),
                 pltpu.VMEM((3, 2, nx, 2, nz), f32),
-                pltpu.VMEM((3, ny, nz), f32),
-                pltpu.VMEM((3, ny, nz), f32),
+                pltpu.VMEM((3, nx, ny, nz), f32),
+                pltpu.VMEM((2, 4 * nz, nz), jnp.bfloat16),
                 pltpu.VMEM((3, nx, nz), f32),
                 pltpu.VMEM((2, 3, nx // sizes[1], nz), f32),
                 pltpu.VMEM((count, 1, nz), f32),
-                dma((2, nx // CHUNK)),
+                dma((2, runs)),
                 dma((nx // CHUNK,)),
-                dma((3, 5)),
-                dma((3, 5)),
+                dma((3, 4)),
+                dma((3, 4)),
+                dma((3, runs)),
+                dma((3, runs)),
                 dma((sizes[1],)),
                 dma((2,)),
                 dma((count,)),

time: 76.7 us -> 49.4 us (0.64)
  Pallas kernels: 72.1 us -> 44.7 us
    pallas_call x1, Pallas kernels: 72.1 us -> 44.7 us  [per_device(): pl.pallas_call(make_kernel(sizes), out_shape=(jax.ShapeDtypeStruct(load.s...]
where the time goes in v2:
time: 49.4 us; the launch traced here: 49.1 us
  Pallas kernels  44.7 us (90%)
  local copies, waits for them, and re-layouts  3.77 us (8%)
  between operations  0.65 us (1%)
    pallas_call x1, Pallas kernels, per_device(): pl.pallas_call(make_kernel(sizes), out_shape=(jax.ShapeDtypeStruct(load.s...  44.7 us
    unnamed x4, local copies, waits for them, and re-layouts  3.77 us

profile of v2, /device:TPU:0, one launch (start us, length us, event | category | flops | bytes accessed | tf_op | source)
XLA Modules:
  0.0 49.1 jit_solution(4735955701601792480)
XLA Ops:
  0.6 44.7 %shard_map.68 = (f32[64,64,128]{2,1,0:T(8,128)}, f32[16,128]{1,0:T(8,128)}) custom-call(f32[64,64,128]{2,1,0:T(8,128)} %load.1, f32[64,64,128]{2,1,0:T(8,128)} %stiff.1, f32[16,128]{1,0:T(8,128)} %pre_ref.1, f32[16,128]{1,0:T(8,128)} %state_ref.1, f32[16,128]{1,0:T(8,128)} %norm_ref.1), custom_call_target="tpu_custom_call" | custom-call | tf_op jit(solution)/shard_map/pallas_call | solution.py:383
  45.3 0.0 copy-start
  45.4 3.2 %copy.9 = f32[64,64,128]{2,1,0:T(8,128)} copy(f32[64,64,128]{2,1,0:T(8,128)} %get-tuple-element.4) | data formatting | bytes 4194304
  48.5 0.0 copy-done
  48.5 0.6 %copy.10 = f32[16,128]{1,0:T(8,128)} copy(f32[16,128]{1,0:T(8,128)S(1)} %copy-done) | data formatting | bytes 16384
Async XLA Ops:
  45.3 3.2 %copy-start = (f32[16,128]{1,0:T(8,128)S(1)}, f32[16,128]{1,0:T(8,128)}, u32[]{:S(2)}) copy-start(f32[16,128]{1,0:T(8,128)} %get-tuple-element.5) | copy-start | bytes 24580

commit v3 on v2

--- a/solution.py
+++ b/solution.py
@@ -56,7 +56,7 @@
     count = ngx * ngy * ngz
 
     def kernel(load, stiff, pre_ref, state_ref, norm_ref, out, slip,
-               b, d, u0, u1, u2, obuf, ysend, yrecv, zrecv, band, fsend, frecv, red,
+               b, d, u0, u1, u2, obuf, ysend, yrecv, zrecv, band, zterm, fsend, frecv, red,
                in_sem, out_sem, send_sem, recv_sem, zs_sem, zr_sem, fs_sem, fr_sem, rs_sem, rr_sem):
         nx, ny, nz = b.shape
         us = (u0, u1, u2)
@@ -132,11 +132,18 @@
                 ysend.at[k, side], yrecv.at[k, 1 - side], send_sem.at[k, 2 + side],
                 recv_sem.at[k, 2 + side], device_id=(ix, to, iz), device_id_type=MESH)
 
-        def zcopy(k, at, size, n):
+        strips = ((8, ny - 8), (0, 8), (ny - 8, ny))
+
+        def zcopy(k, at, size, n, strip):
+            lo, hi = (0, ny) if strip is None else strips[strip]
+            which = 0 if strip is None else strip
             return pltpu.make_async_remote_copy(
-                us[k].at[pl.ds(at + 2, size), PAD:PAD + ny], zrecv.at[k, pl.ds(at, size)],
-                zs_sem.at[k, n], zr_sem.at[k, n],
+                us[k].at[pl.ds(at + 2, size), PAD + lo:PAD + hi], zrecv.at[k, pl.ds(at, size), lo:hi],
+                zs_sem.at[k, n, which], zr_sem.at[k, n, which],
                 device_id=(ix, iy, 1 - iz), device_id_type=MESH)
+
+        def strips_of(n):
+            return (None,) if n < 2 else (0, 1, 2)
 
         def sending(spot, size, side):
             return spot > 0 if side == 0 else spot < size - 1
@@ -175,9 +182,10 @@
             if n == 1:
                 pl.semaphore_wait(barrier, count - 1)
                 start_x(0)
-                zcopy(0, *parts[0], 0).start()
+                zcopy(0, *parts[0], 0, None).start()
             if n >= 1:
-                zcopy(0, at, size, n).start()
+                for strip in strips_of(n):
+                    zcopy(0, at, size, n, strip).start()
         start_y(0)
 
         def wait_y(k):
@@ -186,72 +194,110 @@
         def wait_x(k):
             each(xcopy, k, ix, ngx, receiving, lambda c: c.wait_recv())
 
-        def along_z(k, x, which):
-            own = us[k][pl.ds(x + 2, GROUP), PAD:PAD + ny, :].reshape(GROUP * ny, nz)
-            next_to = zrecv[k, pl.ds(x, GROUP)].reshape(GROUP * ny, nz)
+        def along_z(k, at, size, lo, hi, which):
+            rows = size * (hi - lo)
+            own = us[k][pl.ds(at + 2, size), PAD + lo:PAD + hi, :].reshape(rows, nz)
+            next_to = zrecv[k, pl.ds(at, size), lo:hi, :].reshape(rows, nz)
             own_high, own_low = halves(own)
             next_high, next_low = halves(next_to)
             lhs = jnp.concatenate([own_high, next_high, own_low, next_low], axis=1)
-            return jnp.dot(lhs, band[which], preferred_element_type=jnp.float32)
-
-        def near(k, x, z_term):
+            found = jnp.dot(lhs, band[which], preferred_element_type=jnp.float32)
+            zterm[pl.ds(at, size), lo:hi, :] = found.reshape(size, hi - lo, nz)
+
+        def near(k, x, lo, hi):
             u = us[k]
-            u[x + 2, PAD - 2:PAD, :] = yrecv[k, 0, x]
-            u[x + 2, PAD + ny:PAD + ny + 2, :] = yrecv[k, 1, x]
-            one = (u[x + 1, PAD:PAD + ny, :] + u[x + 3, PAD:PAD + ny, :]
-                   + u[x + 2, PAD - 1:PAD - 1 + ny, :] + u[x + 2, PAD + 1:PAD + 1 + ny, :])
-            two = (u[x, PAD:PAD + ny, :] + u[x + 4, PAD:PAD + ny, :]
-                   + u[x + 2, PAD - 2:PAD - 2 + ny, :] + u[x + 2, PAD + 2:PAD + 2 + ny, :])
-            return (16.0 * one - two + z_term) * (1.0 / 12.0)
-
-        def half_near(k, x, z_term):
+            lo, hi = lo + PAD, hi + PAD
+            one = (u[x + 1, lo:hi, :] + u[x + 3, lo:hi, :]
+                   + u[x + 2, lo - 1:hi - 1, :] + u[x + 2, lo + 1:hi + 1, :])
+            two = (u[x, lo:hi, :] + u[x + 4, lo:hi, :]
+                   + u[x + 2, lo - 2:hi - 2, :] + u[x + 2, lo + 2:hi + 2, :])
+            return (16.0 * one - two + zterm[x, lo - PAD:hi - PAD, :]) * (1.0 / 12.0)
+
+        def half_near(k, x, lo, hi):
             u = us[k]
-            u[x + 2, PAD - 2:PAD, :] = yrecv[k, 0, x]
-            one = u[x + 1, PAD:PAD + ny, :] + u[x + 2, PAD - 1:PAD - 1 + ny, :]
-            two = u[x, PAD:PAD + ny, :] + u[x + 2, PAD - 2:PAD - 2 + ny, :]
-            return (16.0 * one - two + z_term) * (1.0 / 6.0)
+            lo, hi = lo + PAD, hi + PAD
+            one = u[x + 1, lo:hi, :] + u[x + 2, lo - 1:hi - 1, :]
+            two = u[x, lo:hi, :] + u[x + 2, lo - 2:hi - 2, :]
+            return (16.0 * one - two + zterm[x, lo - PAD:hi - PAD, :]) * (1.0 / 6.0)
 
         zero = jnp.zeros((8, nz), jnp.float32)
 
-        def run(plane, k, carry, which, done):
-            def group(at, n, carry):
-                x = at + n * GROUP
-                z_terms = along_z(k, x, which)
+        def run(block, k, carry, which, finish):
+            first_at, size = parts[2]
+
+            def part(n, carry):
+                at = first_at + n * size
+                zcopy(k, at, size, n + 2, 0).wait_recv()
+                along_z(k, at, size, *strips[0], which)
+
+                def inner(i, carry):
+                    for g in range(GROUP):
+                        carry = block(at + i * GROUP + g, *strips[0], carry)
+                    return carry
+
+                carry = lax.fori_loop(0, size // GROUP, inner, carry)
+                if k < 2:
+                    zcopy(k + 1, at, size, n + 2, 0).start()
+                return carry
+
+            carry = lax.fori_loop(0, len(parts) - 2, part, carry)
+            for n, (at, size) in enumerate(parts):
+                for strip in strips_of(n):
+                    if strip != 0:
+                        zcopy(k, at, size, n, strip).wait_recv()
+                if n < 2:
+                    along_z(k, at, size, 0, ny, which)
+            for strip in (1, 2):
+                along_z(k, 2, nx - 4, *strips[strip], which)
+            wait_y(k)
+
+            def rim(i, carry):
                 for g in range(GROUP):
-                    carry = plane(x + g, z_terms[g * ny:(g + 1) * ny], carry)
+                    x = i * GROUP + g
+                    us[k][x + 2, PAD - 2:PAD, :] = yrecv[k, 0, x]
+                    us[k][x + 2, PAD + ny:PAD + ny + 2, :] = yrecv[k, 1, x]
+                    carry = block(x, 0, 8, carry)
+                    carry = block(x, ny - 8, ny, carry)
                 return carry
 
-            def part(at, size, n, carry):
-                zcopy(k, at, size, n).wait_recv()
-                carry = lax.fori_loop(0, size // GROUP, lambda i, c: group(at, i, c), carry)
-                done(at, size, n)
+            def whole(n, carry):
+                x = jnp.where(n < 2, n, nx - 4 + n)
+                us[k][x + 2, PAD - 2:PAD, :] = yrecv[k, 0, x]
+                us[k][x + 2, PAD + ny:PAD + ny + 2, :] = yrecv[k, 1, x]
+                carry = block(x, 0, ny, carry)
                 return carry
 
-            first_at, size = parts[2]
-            carry = lax.fori_loop(
-                0, len(parts) - 2, lambda n, c: part(first_at + n * size, size, n + 2, c), carry)
+            carry = lax.fori_loop(1, nx // GROUP - 1, rim, carry)
             wait_x(k)
-            for n in range(2):
-                carry = part(*parts[n], n, carry)
+            carry = lax.fori_loop(0, 4, whole, carry)
+            finish()
             return carry
 
         def advance(k):
-            def plane(x, z_term, carry):
+            def block(x, lo, hi, carry):
                 even, odd = carry
-                value = us[k][x + 2, PAD:PAD + ny, :]
-                w = near(k, x, z_term)
-                fresh = d[x] * w
-                even = even + total(value * (b[x] - w))
+                value = us[k][x + 2, PAD + lo:PAD + hi, :]
+                w = near(k, x, lo, hi)
+                fresh = d[x, lo:hi, :] * w
+                even = even + total(value * (b[x, lo:hi, :] - w))
                 odd = odd + total((value - fresh) * w)
-                b[x] = w
-                place(x, fresh, k + 1)
+                b[x, lo:hi, :] = w
+                us[k + 1][x + 2, PAD + lo:PAD + hi, :] = fresh
+                if lo == 0:
+                    ysend[k + 1, 0, x] = fresh[0:2]
+                if hi == ny:
+                    ysend[k + 1, 1, x] = fresh[hi - lo - 2:hi - lo]
                 return even, odd
 
-            wait_y(k)
-            even, odd = run(plane, k, (zero, zero), 0, lambda *p: zcopy(k + 1, *p).start())
-            start_x(k + 1)
-            start_y(k + 1)
-            return even, odd
+            def finish():
+                start_x(k + 1)
+                start_y(k + 1)
+                for n, (at, size) in enumerate(parts):
+                    for strip in strips_of(n):
+                        if strip != 0:
+                            zcopy(k + 1, at, size, n, strip).start()
+
+            return run(block, k, (zero, zero), 0, finish)
 
         s0, s1 = advance(0)
         s2, s3 = advance(1)
@@ -285,12 +331,11 @@
                         fault_copy(which, to).start()
                 frecv[which] = fsend[:, owner * owned:(owner + 1) * owned, :]
 
-        def last(x, z_term, s4):
-            value = us[2][x + 2, PAD:PAD + ny, :]
-            return s4 + total(value * (b[x] - half_near(2, x, z_term)))
-
-        wait_y(2)
-        s4 = run(last, 2, zero, 1, lambda *p: None)
+        def last(x, lo, hi, s4):
+            value = us[2][x + 2, PAD + lo:PAD + hi, :]
+            return s4 + total(value * (b[x, lo:hi, :] - half_near(2, x, lo, hi)))
+
+        s4 = run(last, 2, zero, 1, lambda: None)
 
         slot = lax.broadcasted_iota(jnp.int32, (1, nz), 1)
         sent = jnp.zeros((1, nz), jnp.float32)
@@ -348,7 +393,8 @@
             each(xcopy, k, ix, ngx, sending, lambda c: c.wait_send())
             each(ycopy, k, iy, ngy, sending, lambda c: c.wait_send())
             for n, (at, size) in enumerate(parts):
-                zcopy(k, at, size, n).wait_send()
+                for strip in strips_of(n):
+                    zcopy(k, at, size, n, strip).wait_send()
         for which, owner in enumerate((ngy // 2 - 1, ngy // 2)):
             @pl.when(iy == owner)
             def _():
@@ -399,6 +445,7 @@
                 pltpu.VMEM((3, 2, nx, 2, nz), f32),
                 pltpu.VMEM((3, nx, ny, nz), f32),
                 pltpu.VMEM((2, 4 * nz, nz), jnp.bfloat16),
+                pltpu.VMEM((nx, ny, nz), f32),
                 pltpu.VMEM((3, nx, nz), f32),
                 pltpu.VMEM((2, 3, nx // sizes[1], nz), f32),
                 pltpu.VMEM((count, 1, nz), f32),
@@ -406,8 +453,8 @@
                 dma((nx // CHUNK,)),
                 dma((3, 4)),
                 dma((3, 4)),
-                dma((3, runs)),
-                dma((3, runs)),
+                dma((3, runs, 3)),
+                dma((3, runs, 3)),
                 dma((sizes[1],)),
                 dma((2,)),
                 dma((count,)),

time: 49.4 us -> 36.3 us (0.73)
  Pallas kernels: 44.7 us -> 31.6 us
    pallas_call x1, Pallas kernels: 44.7 us -> 31.6 us  [per_device(): pl.pallas_call(make_kernel(sizes), out_shape=(jax.ShapeDtypeStruct(load.s...]
where the time goes in v3:
time: 36.3 us; the launch traced here: 36 us
  Pallas kernels  31.6 us (87%)
  local copies, waits for them, and re-layouts  3.77 us (10%)
  between operations  0.65 us (2%)
    pallas_call x1, Pallas kernels, per_device(): pl.pallas_call(make_kernel(sizes), out_shape=(jax.ShapeDtypeStruct(load.s...  31.6 us
    unnamed x4, local copies, waits for them, and re-layouts  3.77 us

profile of v3, /device:TPU:0, one launch (start us, length us, event | category | flops | bytes accessed | tf_op | source)
XLA Modules:
  0.0 36.0 jit_solution(297664186588866467)
XLA Ops:
  0.6 31.6 %shard_map.68 = (f32[64,64,128]{2,1,0:T(8,128)}, f32[16,128]{1,0:T(8,128)}) custom-call(f32[64,64,128]{2,1,0:T(8,128)} %load.1, f32[64,64,128]{2,1,0:T(8,128)} %stiff.1, f32[16,128]{1,0:T(8,128)} %pre_ref.1, f32[16,128]{1,0:T(8,128)} %state_ref.1, f32[16,128]{1,0:T(8,128)} %norm_ref.1), custom_call_target="tpu_custom_call" | custom-call | tf_op jit(solution)/shard_map/pallas_call | solution.py:429
  32.2 0.0 copy-start
  32.3 3.2 %copy.9 = f32[64,64,128]{2,1,0:T(8,128)} copy(f32[64,64,128]{2,1,0:T(8,128)} %get-tuple-element.4) | data formatting | bytes 4194304
  35.4 0.0 copy-done
  35.4 0.6 %copy.10 = f32[16,128]{1,0:T(8,128)} copy(f32[16,128]{1,0:T(8,128)S(1)} %copy-done) | data formatting | bytes 16384
Async XLA Ops:
  32.2 3.2 %copy-start = (f32[16,128]{1,0:T(8,128)S(1)}, f32[16,128]{1,0:T(8,128)}, u32[]{:S(2)}) copy-start(f32[16,128]{1,0:T(8,128)} %get-tuple-element.5) | copy-start | bytes 24580

commit v4 on v3

--- a/solution.py
+++ b/solution.py
@@ -55,9 +55,9 @@
     ngx, ngy, ngz = sizes
     count = ngx * ngy * ngz
 
-    def kernel(load, stiff, pre_ref, state_ref, norm_ref, out, slip,
-               b, d, u0, u1, u2, obuf, ysend, yrecv, zrecv, band, zterm, fsend, frecv, red,
-               in_sem, out_sem, send_sem, recv_sem, zs_sem, zr_sem, fs_sem, fr_sem, rs_sem, rr_sem):
+    def kernel(load, stiff, pre_ref, state_ref, norm_ref, u0, u1, u2, coef_ref, slip,
+               b, d, ysend, yrecv, zrecv, band, zterm, fsend, frecv, red,
+               in_sem, send_sem, recv_sem, zs_sem, zr_sem, fs_sem, fr_sem, rs_sem, rr_sem):
         nx, ny, nz = b.shape
         us = (u0, u1, u2)
         ix, iy, iz = (lax.axis_index(a) for a in AXES)
@@ -364,19 +364,8 @@
         sums = [jnp.sum(jnp.where(slot == j, sums, 0.0), axis=1, keepdims=True) for j in range(6)]
         coefs = [jnp.broadcast_to(c, (1, nz)) for c in solve(sums[0], sums[1:])]
 
-        def out_copy(c):
-            part = pl.ds(c * CHUNK, CHUNK)
-            return pltpu.make_async_copy(obuf.at[part], out.at[part], out_sem.at[c])
-
-        def blend(x, carry):
-            mid = slice(PAD, PAD + ny)
-            obuf[x] = (coefs[0] * u0[x + 2, mid, :] + coefs[1] * u1[x + 2, mid, :]
-                       + coefs[2] * u2[x + 2, mid, :])
-            return carry
-
-        for c in range(nx // CHUNK):
-            lax.fori_loop(c * CHUNK, (c + 1) * CHUNK, blend, 0)
-            out_copy(c).start()
+        for j in range(3):
+            coef_ref[j:j + 1, :] = coefs[j]
 
         for which, owner in enumerate((ngy // 2 - 1, ngy // 2)):
             @pl.when(iy != owner)
@@ -406,10 +395,28 @@
         def _(step):
             sum_copy(step).wait_send()
 
-        for c in range(nx // CHUNK):
-            out_copy(c).wait()
-
     return kernel
+
+
+def blend(u0, u1, u2, coef_ref, out, obuf, out_sem):
+    nx, ny, nz = obuf.shape
+    mid = slice(PAD, PAD + ny)
+    coefs = [coef_ref[j:j + 1, :] for j in range(3)]
+
+    def out_copy(c):
+        part = pl.ds(c * CHUNK, CHUNK)
+        return pltpu.make_async_copy(obuf.at[part], out.at[part], out_sem.at[c])
+
+    def plane(x, carry):
+        obuf[x] = (coefs[0] * u0[x + 2, mid, :] + coefs[1] * u1[x + 2, mid, :]
+                   + coefs[2] * u2[x + 2, mid, :])
+        return carry
+
+    for c in range(nx // CHUNK):
+        lax.fori_loop(c * CHUNK, (c + 1) * CHUNK, plane, 0)
+        out_copy(c).start()
+    for c in range(nx // CHUNK):
+        out_copy(c).wait()
 
 
 def solution(mesh):
@@ -424,22 +431,21 @@
         count = sizes[0] * sizes[1] * sizes[2]
         padded = (nx + 4, ny + 2 * PAD, nz)
         vmem = pl.BlockSpec(memory_space=pltpu.VMEM)
-        hbm = pl.BlockSpec(memory_space=pl.ANY)
+        hbm = pl.BlockSpec(memory_space=pltpu.HBM)
         dma = pltpu.SemaphoreType.DMA
-        return pl.pallas_call(
+        u0, u1, u2, coefs, slip = pl.pallas_call(
             make_kernel(sizes),
             out_shape=(
-                jax.ShapeDtypeStruct(load.shape, f32),
+                pltpu.VMEM(padded, f32),
+                pltpu.VMEM(padded, f32),
+                pltpu.VMEM(padded, f32),
+                pltpu.VMEM((8, nz), f32),
                 jax.ShapeDtypeStruct(prestress.shape, f32),
             ),
             in_specs=[hbm, hbm, vmem, vmem, vmem],
-            out_specs=(hbm, vmem),
+            out_specs=(vmem,) * 5,
             scratch_shapes=[
                 pltpu.VMEM((nx, ny, nz), f32),
-                pltpu.VMEM((nx, ny, nz), f32),
-                pltpu.VMEM(padded, f32),
-                pltpu.VMEM(padded, f32),
-                pltpu.VMEM(padded, f32),
                 pltpu.VMEM((nx, ny, nz), f32),
                 pltpu.VMEM((3, 2, nx, 2, nz), f32),
                 pltpu.VMEM((3, 2, nx, 2, nz), f32),
@@ -450,7 +456,6 @@
                 pltpu.VMEM((2, 3, nx // sizes[1], nz), f32),
                 pltpu.VMEM((count, 1, nz), f32),
                 dma((2, runs)),
-                dma((nx // CHUNK,)),
                 dma((3, 4)),
                 dma((3, 4)),
                 dma((3, runs, 3)),
@@ -460,8 +465,18 @@
                 dma((count,)),
                 dma((count,)),
             ],
-            compiler_params=pltpu.CompilerParams(collective_id=0, has_side_effects=True),
+            compiler_params=pltpu.CompilerParams(
+                collective_id=0, has_side_effects=True, vmem_limit_bytes=54 * 2**20),
         )(load, stiffness, prestress, state_var, normal_a)
+        displacement = pl.pallas_call(
+            blend,
+            out_shape=jax.ShapeDtypeStruct(load.shape, f32),
+            in_specs=[vmem] * 4,
+            out_specs=hbm,
+            scratch_shapes=[pltpu.VMEM((nx, ny, nz), f32), dma((nx // CHUNK,))],
+            compiler_params=pltpu.CompilerParams(vmem_limit_bytes=8 * 2**20),
+        )(u0, u1, u2, coefs)
+        return displacement, slip
 
     placed = (
         P("gx", "gy", "gz"),

time: 36.3 us -> 33.5 us (0.923)
  local copies, waits for them, and re-layouts: 3.77 us -> 0.61 us
  Pallas kernels: 31.6 us -> 32 us
    unnamed x4 -> x3, local copies, waits for them, and re-layouts: 3.77 us -> 0.61 us
    pallas_call x1 -> x2, Pallas kernels: 31.6 us -> 32 us  [the longest x1 30.5 us: per_device(): pl.pallas_call(make_kernel(sizes), out_shape=(pltpu.VMEM(padded, f32), pl...]
where the time goes in v4:
time: 33.5 us; the launch traced here: 33.3 us
  Pallas kernels  32 us (96%)
  between operations  0.66 us (2%)
  local copies, waits for them, and re-layouts  0.61 us (2%)
    pallas_call x1, Pallas kernels, per_device(): pl.pallas_call(make_kernel(sizes), out_shape=(pltpu.VMEM(padded, f32), pl...  30.5 us
    pallas_call x1, Pallas kernels, per_device(): pl.pallas_call(blend, out_shape=jax.ShapeDtypeStruct(load.shape, f32), in...  1.49 us

profile of v4, /device:TPU:0, one launch (start us, length us, event | category | flops | bytes accessed | tf_op | source)
XLA Modules:
  0.0 33.3 jit_solution(2097898246388389012)
XLA Ops:
  0.6 30.5 %shard_map.68 = (f32[68,80,128]{2,1,0:T(8,128)S(1)}, f32[68,80,128]{2,1,0:T(8,128)S(1)}, f32[68,80,128]{2,1,0:T(8,128)S(1)}, f32[8,128]{1,0:T(8,128)S(1)}, f32[16,128]{1,0:T(8,128)}) custom-call(f32[64,64,128]{2,1,0:T(8,128)} %load.1, f32[64,64,128]{2,1,0:T(8,128)} %stiff.1, f32[16,128]{1,0:T(8,128)} %pre_ref.1, f32[16,128]{1,0:T(8,128)} %state_ref.1, ...), custom_call_target="tpu_custom_call" | custom-call | tf_op jit(solution)/shard_map/pallas_call | solution.py:436
  31.1 0.0 copy-start
  31.2 1.5 %shard_map.69 = f32[64,64,128]{2,1,0:T(8,128)} custom-call(f32[68,80,128]{2,1,0:T(8,128)S(1)} %get-tuple-element.7.u0, f32[68,80,128]{2,1,0:T(8,128)S(1)} %get-tuple-element.8.u1, f32[68,80,128]{2,1,0:T(8,128)S(1)} %get-tuple-element.9.u2, f32[8,128]{1,0:T(8,128)S(1)} %get-tuple-element.10.coef_ref), custom_call_target="tpu_custom_call" | custom-call | tf_op jit(solution)/shard_map/pallas_call | solution.py:471
  32.6 0.0 copy-done
  32.7 0.6 %copy.8 = f32[16,128]{1,0:T(8,128)} copy(f32[16,128]{1,0:T(8,128)S(1)} %copy-done) | data formatting | bytes 16384
Async XLA Ops:
  31.1 1.5 %copy-start = (f32[16,128]{1,0:T(8,128)S(1)}, f32[16,128]{1,0:T(8,128)}, u32[]{:S(2)}) copy-start(f32[16,128]{1,0:T(8,128)} %get-tuple-element.15) | copy-start | bytes 24580
